TPU v7x, 32 devices: a whole 2x2x4 slice. The times are simulated.
32 devices in a mesh: wide: 16 (over z, x, core), narrow: 2 (over y).
Axes of the slice: x: 2, y: 2, z: 4, core: 2. Of those that a mesh axis runs over, the one named last changes fastest.
Arguments:
- tokens: bfloat16 [2, 32768, 768], P(None, ('wide', 'narrow')), may hold values from -6 to 6
- grad_out: bfloat16 [2, 32768, 768], P(None, ('wide', 'narrow')), may hold values from -6 to 6
- route_ids: int32 [2, 32768], P(None, ('wide', 'narrow')), may hold values from 0 to 15, as said below
- slot_ids: int32 [2, 32768], P(None, ('wide', 'narrow')), may hold values from 0 to 63, as said below
- keep_ids: int32 [2, 32768], P(None, ('wide', 'narrow')), may hold values from 0 to 1, as said below
- gain_one: float32 [768], replicated, may hold values from 0.5 to 1.5
- w_query: bfloat16 [768, 768], replicated, may hold values from -0.21875 to 0.21875
- w_key: bfloat16 [768, 768], replicated, may hold values from -0.21875 to 0.21875
- w_value: bfloat16 [768, 768], replicated, may hold values from -0.21875 to 0.21875
- w_out: bfloat16 [768, 768], replicated, may hold values from -4 to 4
- gain_two: float32 [768], replicated, may hold values from 0.5 to 1.5
- w_route: bfloat16 [768, 16], replicated, may hold values from -0.21875 to 0.21875
- embed: float32 [16, 16], replicated, may hold values from -6 to 6
- w_in: bfloat16 [16, 768, 3072], P('wide', None, 'narrow'), may hold values from -0.21875 to 0.21875
- w_outer: bfloat16 [16, 3072, 768], P('wide', 'narrow'), may hold values from -1.75 to 1.75
Outputs:
- block_out: bfloat16 [2, 32768, 768], P(None, ('wide', 'narrow'))
- grad_tokens: bfloat16 [2, 32768, 768], P(None, ('wide', 'narrow'))
- grad_gain_one: float32 [768], replicated
- grad_w_query: float32 [768, 768], replicated
- grad_w_key: float32 [768, 768], replicated
- grad_w_value: float32 [768, 768], replicated
- grad_w_out: float32 [768, 768], replicated
- grad_gain_two: float32 [768], replicated
- grad_w_route: float32 [768, 16], replicated
- grad_embed: float32 [16, 16], replicated
- grad_w_in: float32 [16, 768, 3072], P('wide', None, 'narrow')
- grad_w_outer: float32 [16, 3072, 768], P('wide', 'narrow')
Inputs may be any that keep to these rules, and one draw needn't show every extreme that they name: `route_ids`: an expert's number for every token. `slot_ids`: within one aligned block of 1024 tokens of a micro-batch, the kept tokens bound for one expert carry slots 0, 1, 2, ... in token order; a token that would need slot 64 or more is dropped and carries 0. In every block some expert has all 64 slots filled and more tokens than that. `keep_ids`: 1 exactly for the tokens that got a slot; tokens are dropped in token order once an expert's 64 slots of the block are taken.
All inputs are finite; a program needn't handle non-finite values.
Results may differ from a plain program's by a relative error of at most 0.015.
Values may be sent and summed in bfloat16 or wider, within the bound.
A program may use at most 384 MiB of HBM per device.

v0:
```python
import jax
import jax.numpy as jnp
from jax import lax
from jax.sharding import PartitionSpec as P

D = 768
HEADS = 12
HEAD_DIM = 64
LENGTH = 1024


def layer_norm(values, gain_vec):
    centred = values - jnp.mean(values, axis=-1, keepdims=True)
    spread_sq = jnp.mean(centred * centred, axis=-1, keepdims=True)
    return centred * lax.rsqrt(spread_sq + 1e-05) * gain_vec


def gate_from(projected, embed_rows, route_row):
    unit_rows = projected * lax.rsqrt(jnp.sum(projected * projected, axis=-1, keepdims=True) + 1.0)
    anchor = embed_rows * lax.rsqrt(jnp.sum(embed_rows * embed_rows, axis=-1, keepdims=True) + 1.0)
    logits = 3.0 * jnp.dot(
        unit_rows, anchor.T, precision=lax.Precision.HIGHEST, preferred_element_type=jnp.float32
    )
    soft_rows = jax.nn.softmax(logits, axis=-1)
    picked = route_row[:, None] == jnp.arange(soft_rows.shape[1], dtype=jnp.int32)[None, :]
    return jnp.sum(jnp.where(picked, soft_rows, 0.0), axis=-1)


def contract_rows(left, right, precise=None):
    return lax.dot_general(
        left, right, (((0,), (0,)), ((), ())), precision=precise, preferred_element_type=jnp.float32
    )


def contract_cols(left, right, precise=None):
    return lax.dot_general(
        left, right, (((1,), (1,)), ((), ())), precision=precise, preferred_element_type=jnp.float32
    )


def gelu_exact(values):
    return jax.nn.gelu(values, approximate=False)


def split_heads(flat_rows):
    return flat_rows.reshape(flat_rows.shape[0] // LENGTH, LENGTH, HEADS, HEAD_DIM)


def attention_forward(qkv_rows):
    tok_count = qkv_rows.shape[0]
    block_rows = min(512, LENGTH)
    count_blocks = LENGTH // block_rows
    score_scale = HEAD_DIM ** (-0.5)
    queries = split_heads(qkv_rows[:, :D])
    keys_in = split_heads(qkv_rows[:, D : 2 * D])
    values_in = split_heads(qkv_rows[:, 2 * D :])

    def one_block(row_start):
        query_block = lax.dynamic_slice_in_dim(queries, row_start, block_rows, 1)
        scores = (
            jnp.einsum("sqhd,skhd->shqk", query_block, keys_in, preferred_element_type=jnp.float32)
            * score_scale
        )
        row_max = jnp.max(scores, axis=-1, keepdims=True)
        exp_scores = jnp.exp(scores - row_max)
        row_total = jnp.sum(exp_scores, axis=-1, keepdims=True)
        soft_weights = (exp_scores / row_total).astype(jnp.bfloat16)
        mixed_block = jnp.einsum(
            "shqk,skhd->sqhd", soft_weights, values_in, preferred_element_type=jnp.float32
        )
        return (mixed_block.astype(jnp.bfloat16), (row_max + jnp.log(row_total))[..., 0])

    starts = jnp.arange(count_blocks, dtype=jnp.int32) * block_rows
    mixed_blocks, log_totals = lax.map(one_block, starts)
    mixed_rows = jnp.moveaxis(mixed_blocks, 0, 1).reshape(tok_count, D)
    return (mixed_rows, log_totals)


def attention_backward(qkv_rows, log_totals, grad_mixed):
    tok_count = qkv_rows.shape[0]
    block_rows = min(512, LENGTH)
    count_blocks = LENGTH // block_rows
    score_scale = HEAD_DIM ** (-0.5)
    queries = split_heads(qkv_rows[:, :D])
    keys_in = split_heads(qkv_rows[:, D : 2 * D])
    values_in = split_heads(qkv_rows[:, 2 * D :])
    grad_heads = split_heads(grad_mixed)

    def one_block(carry, block_index):
        grad_keys, grad_values = carry
        row_start = block_index * block_rows
        query_block = lax.dynamic_slice_in_dim(queries, row_start, block_rows, 1)
        grad_block = lax.dynamic_slice_in_dim(grad_heads, row_start, block_rows, 1)
        scores = (
            jnp.einsum("sqhd,skhd->shqk", query_block, keys_in, preferred_element_type=jnp.float32)
            * score_scale
        )
        soft_weights = jnp.exp(scores - log_totals[block_index][..., None])
        grad_soft = jnp.einsum(
            "sqhd,skhd->shqk", grad_block, values_in, preferred_element_type=jnp.float32
        )
        inner_term = jnp.sum(soft_weights * grad_soft, axis=-1, keepdims=True)
        grad_scores = (soft_weights * (grad_soft - inner_term)).astype(jnp.bfloat16)
        grad_query = (
            jnp.einsum("shqk,skhd->sqhd", grad_scores, keys_in, preferred_element_type=jnp.float32)
            * score_scale
        )
        grad_keys = (
            grad_keys
            + jnp.einsum(
                "shqk,sqhd->skhd", grad_scores, query_block, preferred_element_type=jnp.float32
            )
            * score_scale
        )
        grad_values = grad_values + jnp.einsum(
            "shqk,sqhd->skhd",
            soft_weights.astype(jnp.bfloat16),
            grad_block,
            preferred_element_type=jnp.float32,
        )
        return ((grad_keys, grad_values), grad_query)

    zero_heads = jnp.zeros(queries.shape, jnp.float32)
    (grad_keys, grad_values), grad_queries = lax.scan(
        one_block, (zero_heads, zero_heads), jnp.arange(count_blocks, dtype=jnp.int32)
    )
    grad_queries = jnp.moveaxis(grad_queries, 0, 1).reshape(tok_count, D)
    joined = jnp.concatenate(
        [grad_queries, grad_keys.reshape(tok_count, D), grad_values.reshape(tok_count, D)], axis=1
    )
    return joined.astype(jnp.bfloat16)


def local(
    tokens,
    grad_out,
    route_ids,
    slot_ids,
    keep_ids,
    gain_one,
    w_query,
    w_key,
    w_value,
    w_out,
    gain_two,
    w_route,
    embed,
    w_in,
    w_outer,
):
    micro_count, tok_count, feat_width = tokens.shape
    wide_count = lax.axis_size("wide")
    expert_count = embed.shape[0]
    slot_cap = max(2, tok_count // expert_count)
    w_qkv = jnp.concatenate([w_query, w_key, w_value], axis=1)
    route_float = w_route.astype(jnp.float32)
    local_in = w_in[0]
    local_outer = w_outer[0]
    acc_in = jnp.zeros(local_in.shape, jnp.float32)
    acc_outer = jnp.zeros(local_outer.shape, jnp.float32)
    acc_gain_one = jnp.zeros(gain_one.shape, jnp.float32)
    acc_qkv = jnp.zeros(w_qkv.shape, jnp.float32)
    acc_wo = jnp.zeros(w_out.shape, jnp.float32)
    acc_gain_two = jnp.zeros(gain_two.shape, jnp.float32)
    acc_route = jnp.zeros(w_route.shape, jnp.float32)
    acc_embed = jnp.zeros(embed.shape, jnp.float32)
    outputs = []
    input_grads = []
    slot_columns = jnp.arange(expert_count * slot_cap, dtype=jnp.int32)
    for micro_step in range(micro_count):
        route_row = route_ids[micro_step]
        inputs = tokens[micro_step].astype(jnp.float32)
        normed_one, pull_one = jax.vjp(layer_norm, inputs, gain_one)
        normed_low = normed_one.astype(jnp.bfloat16)
        qkv_rows = jnp.dot(normed_low, w_qkv, preferred_element_type=jnp.float32).astype(
            jnp.bfloat16
        )
        mixed_rows, log_totals = attention_forward(qkv_rows)
        first_sum = inputs + jnp.dot(mixed_rows, w_out, preferred_element_type=jnp.float32)
        normed_two, pull_two = jax.vjp(layer_norm, first_sum, gain_two)
        second_low = normed_two.astype(jnp.bfloat16)
        projected = jnp.dot(second_low, w_route, preferred_element_type=jnp.float32)
        gate_prob, pull_gate = jax.vjp(
            lambda proj_in, embed_in: gate_from(proj_in, embed_in, route_row), projected, embed
        )
        slot_index = jnp.where(
            keep_ids[micro_step] > 0, route_row * slot_cap + slot_ids[micro_step], -1
        )
        slot_table = (slot_index[:, None] == slot_columns[None, :]).astype(jnp.bfloat16)
        sent_rows = (
            contract_rows(slot_table, second_low)
            .astype(jnp.bfloat16)
            .reshape(expert_count, slot_cap, feat_width)
        )
        arrived = lax.all_to_all(
            sent_rows, "wide", split_axis=0, concat_axis=0, tiled=True
        ).reshape(-1, feat_width)
        all_rows = lax.all_gather(arrived, "narrow", axis=0, tiled=True)
        pre_act = jnp.dot(all_rows, local_in, preferred_element_type=jnp.float32)
        hidden = gelu_exact(pre_act).astype(jnp.bfloat16)
        partial_rows = jnp.dot(hidden, local_outer, preferred_element_type=jnp.float32)
        result_rows = lax.psum_scatter(
            partial_rows.astype(jnp.bfloat16), "narrow", scatter_dimension=0, tiled=True
        )
        back_rows = lax.all_to_all(
            result_rows.reshape(wide_count, slot_cap, feat_width),
            "wide",
            split_axis=0,
            concat_axis=0,
            tiled=True,
        )
        returned = jnp.dot(
            slot_table, back_rows.reshape(-1, feat_width), preferred_element_type=jnp.float32
        )
        block_sum = first_sum + gate_prob[:, None] * returned
        outputs.append(block_sum.astype(jnp.bfloat16))
        grad_sum = grad_out[micro_step].astype(jnp.float32)
        grad_gate = jnp.sum(grad_sum * returned, axis=-1)
        grad_returned = (gate_prob[:, None] * grad_sum).astype(jnp.bfloat16)
        grad_buffer = (
            contract_rows(slot_table, grad_returned)
            .astype(jnp.bfloat16)
            .reshape(expert_count, slot_cap, feat_width)
        )
        grad_result = lax.all_to_all(
            grad_buffer, "wide", split_axis=0, concat_axis=0, tiled=True
        ).reshape(-1, feat_width)
        grad_all = lax.all_gather(grad_result, "narrow", axis=0, tiled=True)
        acc_outer = acc_outer + contract_rows(hidden, grad_all)
        grad_hidden = contract_cols(grad_all, local_outer)
        grad_pre = jax.vjp(gelu_exact, pre_act)[1](grad_hidden)[0].astype(jnp.bfloat16)
        acc_in = acc_in + contract_rows(all_rows, grad_pre)
        grad_part = contract_cols(grad_pre, local_in)
        grad_arrived = lax.psum_scatter(
            grad_part.astype(jnp.bfloat16), "narrow", scatter_dimension=0, tiled=True
        )
        grad_sent = lax.all_to_all(
            grad_arrived.reshape(wide_count, slot_cap, feat_width),
            "wide",
            split_axis=0,
            concat_axis=0,
            tiled=True,
        )
        grad_second = jnp.dot(
            slot_table, grad_sent.reshape(-1, feat_width), preferred_element_type=jnp.float32
        )
        grad_projected, grad_embed_part = pull_gate(grad_gate)
        grad_second = grad_second + contract_cols(
            grad_projected, route_float, lax.Precision.HIGHEST
        )
        acc_route = acc_route + contract_rows(
            second_low.astype(jnp.float32), grad_projected, lax.Precision.HIGHEST
        )
        acc_embed = acc_embed + grad_embed_part
        grad_first_norm, grad_gain_b = pull_two(grad_second)
        acc_gain_two = acc_gain_two + grad_gain_b
        grad_first = grad_sum + grad_first_norm
        grad_branch = grad_first.astype(jnp.bfloat16)
        acc_wo = acc_wo + contract_rows(mixed_rows, grad_branch)
        grad_mixed = contract_cols(grad_branch, w_out).astype(jnp.bfloat16)
        grad_qkv = attention_backward(qkv_rows, log_totals, grad_mixed)
        acc_qkv = acc_qkv + contract_rows(normed_low, grad_qkv)
        grad_normed = contract_cols(grad_qkv, w_qkv)
        grad_input_norm, grad_gain_a = pull_one(grad_normed)
        acc_gain_one = acc_gain_one + grad_gain_a
        input_grads.append((grad_first + grad_input_norm).astype(jnp.bfloat16))
    sum_gain_one, sum_qkv, sum_wo, sum_gain_two, sum_route, sum_embed = lax.psum(
        (acc_gain_one, acc_qkv, acc_wo, acc_gain_two, acc_route, acc_embed), ("wide", "narrow")
    )
    grad_in_local, grad_outer_local = (acc_in, acc_outer)
    return (
        jnp.stack(outputs),
        jnp.stack(input_grads),
        sum_gain_one,
        sum_qkv[:, :feat_width],
        sum_qkv[:, feat_width : 2 * feat_width],
        sum_qkv[:, 2 * feat_width :],
        sum_wo,
        sum_gain_two,
        sum_route,
        sum_embed,
        grad_in_local[None],
        grad_outer_local[None],
    )


def solution(mesh):
    placed = (
        P(None, ("wide", "narrow"), None),
        P(None, ("wide", "narrow"), None),
        P(None, ("wide", "narrow")),
        P(None, ("wide", "narrow")),
        P(None, ("wide", "narrow")),
        P(),
        P(),
        P(),
        P(),
        P(),
        P(),
        P(),
        P(),
        P("wide", None, "narrow"),
        P("wide", "narrow", None),
    )
    return jax.shard_map(
        local,
        mesh=mesh,
        in_specs=placed,
        out_specs=(
            P(None, ("wide", "narrow"), None),
            P(None, ("wide", "narrow"), None),
            P(),
            P(),
            P(),
            P(),
            P(),
            P(),
            P(),
            P(),
            P("wide", None, "narrow"),
            P("wide", "narrow", None),
        ),
        check_vma=False,
    )
```

profile of v0, /device:TPU:0, one launch (start us, length us, event | category | flops | bytes accessed | tf_op | source)
XLA Modules:
  0.0 1653.0 jit_solution(5152117024401113663)
XLA Ops:
  45.7 78.8 %while.55 = (s32[]{:T(128)}, bf16[2,1,512,12,64]{2,4,3,1,0:T(8,128)(2,1)}, f32[2,1,12,512]{3,2,1,0:T(8,128)S(1)}, s32[2]{0:T(128)S(1)}, bf16[1,1024,12,64]{1,3,2...) while((s32[]{:T(128)}, ...), condition=%wide.region_19.20_spmd, body=%wide.region_16.19_spmd.sunk | while | flops 1667622912 | bytes 99328248 | solution.py:74
  148.7 78.6 %while.54 = (s32[]{:T(128)}, bf16[2,1,512,12,64]{2,4,3,1,0:T(8,128)(2,1)}, f32[2,1,12,512]{3,2,1,0:T(8,128)S(1)}, s32[2]{0:T(128)S(1)}, bf16[1,1024,12,64]{1,3,2...) while((s32[]{:T(128)}, ...), condition=%wide.region_5.6_spmd, body=%wide.region_2.5_spmd.sunk | while | flops 1667622912 | bytes 99328248 | solution.py:74
  238.2 43.2 %all_to_all.40 = bf16[16,64,768]{2,1,0:T(8,128)(2,1)} all-to-all(bf16[16,64,768]{2,1,0:T(8,128)(2,1)S(1)} %bitcast.480), channel_id=1, replica_groups=mesh['wide'=16,'narrow'=2] {'wide'}, dimensions={0} | all-to-all | bytes 3145728 | tf_op jit(solution)/shard_map/all_to_all | solution.py:195
  281.4 45.5 %all-gather.5.cloned.1.call-done = bf16[2048,768]{1,0:T(8,128)(2,1)} async-done(((bf16[1024,768]{1,0:T(8,128)(2,1)}), bf16[2048,768]{1,0:T(8,128)(2,1)}) %all-gather.5.cloned.1.call-update) | async-done | bytes 3145744 | tf_op jit(solution)/shard_map/all_gather | solution.py:198
  326.9 33.7 %multiply_convert_fusion.3 = (bf16[2048,1536]{1,0:T(8,128)(2,1)S(1)}, f32[2048,1536]{1,0:T(8,128)}, f32[2048,1536]{1,0:T(8,128)}) fusion(bf16[2048,768]{1,0:T(8,128)(2,1)} %all-gather.5.cloned.1.call-done, bf16[1,768,1536]{2,1,0:T(8,128)(2,1)S(1)} %copy-done), kind=kOutput, calls=%fused_computation.111 | convolution fusion | flops 5036310528 | bytes 36962304 | tf_op jit(solution)/shard_map/dot_general | solution.py:199
  369.6 43.6 %reduce-scatter.5.cloned.1.call-done = bf16[1024,768]{1,0:T(8,128)(2,1)} async-done(((bf16[2048,768]{1,0:T(8,128)(2,1)}), bf16[1024,768]{1,0:T(8,128)(2,1)}) %reduce-scatter.5.cloned.1.call-update) | async-done | bytes 1572880 | tf_op jit(solution)/shard_map/reduce_scatter | solution.py:202
  427.6 23.2 %all-to-all-done.1 = bf16[16,64,768]{2,1,0:T(8,128)(2,1)} async-done(((bf16[16,64,768]{2,1,0:T(8,128)(2,1)}), bf16[16,64,768]{2,1,0:T(8,128)(2,1)}, u32[]{:S(2)}, u32[]{:S(2)}) %all-to-all-start.1) | async-done | bytes 1572896 | tf_op jit(solution)/shard_map/all_to_all | solution.py:205
  458.6 44.9 %all_to_all.41 = bf16[16,64,768]{2,1,0:T(8,128)(2,1)} all-to-all(bf16[16,64,768]{2,1,0:T(8,128)(2,1)S(1)} %bitcast.481), channel_id=1, replica_groups=mesh['wide'=16,'narrow'=2] {'wide'}, dimensions={0} | all-to-all | bytes 3145728 | tf_op jit(solution)/shard_map/all_to_all | solution.py:225
  503.6 44.5 %all-gather.9.cloned.1.call-done = bf16[2048,768]{1,0:T(8,128)(2,1)} async-done(((bf16[1024,768]{1,0:T(8,128)(2,1)}), bf16[2048,768]{1,0:T(8,128)(2,1)}) %all-gather.9.cloned.1.call-update) | async-done | bytes 3145744 | tf_op jit(solution)/shard_map/all_gather | solution.py:228
  573.7 43.6 %reduce-scatter.9.cloned.1.call-done = bf16[1024,768]{1,0:T(8,128)(2,1)} async-done(((bf16[2048,768]{1,0:T(8,128)(2,1)}), bf16[1024,768]{1,0:T(8,128)(2,1)}) %reduce-scatter.9.cloned.1.call-update) | async-done | bytes 1572880 | tf_op jit(solution)/shard_map/reduce_scatter | solution.py:234
  623.6 31.2 %all-to-all-done.5 = bf16[16,64,768]{2,1,0:T(8,128)(2,1)} async-done(((bf16[16,64,768]{2,1,0:T(8,128)(2,1)}), bf16[16,64,768]{2,1,0:T(8,128)(2,1)}, u32[]{:S(2)}, u32[]{:S(2)}) %all-to-all-start.5) | async-done | bytes 1572896 | tf_op jit(solution)/shard_map/all_to_all | solution.py:237
  667.7 44.9 %all_to_all.42 = bf16[16,64,768]{2,1,0:T(8,128)(2,1)} all-to-all(bf16[16,64,768]{2,1,0:T(8,128)(2,1)S(1)} %bitcast.482), channel_id=1, replica_groups=mesh['wide'=16,'narrow'=2] {'wide'}, dimensions={0} | all-to-all | bytes 3145728 | tf_op jit(solution)/shard_map/all_to_all | solution.py:195
  712.7 44.5 %all-gather.7.cloned.1.call-done = bf16[2048,768]{1,0:T(8,128)(2,1)} async-done(((bf16[1024,768]{1,0:T(8,128)(2,1)}), bf16[2048,768]{1,0:T(8,128)(2,1)}) %all-gather.7.cloned.1.call-update) | async-done | bytes 3145744 | tf_op jit(solution)/shard_map/all_gather | solution.py:198
  757.2 33.5 %multiply_convert_fusion.2 = (bf16[2048,1536]{1,0:T(8,128)(2,1)S(1)}, f32[2048,1536]{1,0:T(8,128)}, f32[2048,1536]{1,0:T(8,128)}) fusion(bf16[2048,768]{1,0:T(8,128)(2,1)} %all-gather.7.cloned.1.call-done, bf16[1,768,1536]{2,1,0:T(8,128)(2,1)S(1)} %copy-done), kind=kOutput, calls=%fused_computation.98 | convolution fusion | flops 5036310528 | bytes 36962304 | tf_op jit(solution)/shard_map/dot_general | solution.py:199
  799.8 43.6 %reduce-scatter.7.cloned.1.call-done = bf16[1024,768]{1,0:T(8,128)(2,1)} async-done(((bf16[2048,768]{1,0:T(8,128)(2,1)}), bf16[1024,768]{1,0:T(8,128)(2,1)}) %reduce-scatter.7.cloned.1.call-update) | async-done | bytes 1572880 | tf_op jit(solution)/shard_map/reduce_scatter | solution.py:202
  854.3 26.6 %all-to-all-done.3 = bf16[16,64,768]{2,1,0:T(8,128)(2,1)} async-done(((bf16[16,64,768]{2,1,0:T(8,128)(2,1)}), bf16[16,64,768]{2,1,0:T(8,128)(2,1)}, u32[]{:S(2)}, u32[]{:S(2)}) %all-to-all-start.3) | async-done | bytes 1572896 | tf_op jit(solution)/shard_map/all_to_all | solution.py:205
  903.1 28.4 %all-to-all-done.6 = bf16[16,64,768]{2,1,0:T(8,128)(2,1)} async-done(((bf16[16,64,768]{2,1,0:T(8,128)(2,1)}), bf16[16,64,768]{2,1,0:T(8,128)(2,1)}, u32[]{:S(2)}, u32[]{:S(2)}) %all-to-all-start.6) | async-done | bytes 1572896 | tf_op jit(solution)/shard_map/all_to_all | solution.py:225
  956.5 23.7 %all-gather.11.cloned.1.call-done = bf16[2048,768]{1,0:T(8,128)(2,1)} async-done(((bf16[1024,768]{1,0:T(8,128)(2,1)}), bf16[2048,768]{1,0:T(8,128)(2,1)}) %all-gather.11.cloned.1.call-update) | async-done | bytes 3145744 | tf_op jit(solution)/shard_map/all_gather | solution.py:228
  1007.3 170.1 %while.56 = (s32[]{:T(128)}, f32[1,1024,12,64]{1,3,2,0:T(8,128)}, f32[1,1024,12,64]{1,3,2,0:T(8,128)}, bf16[2,1,512,12,64]{2,4,3,1,0:T(8,128)(2,1)}, s32[2]{0:T(...) while((s32[]{:T(128)}, f32[1,1024,12,64]{1,3,2,0:T(8,128)}, ...), condition=%wide.region_35.36_spmd.clone, body=%wide.region_33.35_spmd.clone.sunk | while | flops 4106348544 | bytes 217235760 | solution.py:124
  1052.1 21.5 %multiply_convert_fusion.8 = bf16[12,512,1024]{2,1,0:T(8,128)(2,1)} fusion(f32[12,512,1024]{2,1,0:T(8,128)} %get-tuple-element.703, f32[12,512,1024]{2,1,0:T(8,128)} %fusion.350, f32[12,512]{1,0:T(8,128)S(1)} %get-tuple-element.704, f32[12,512]{1,0:T(8,128)S(1)} %dynamic-slice_bitcast_fusion.4), kind=kLoop, calls=%fused_computation.32.clone.1 | loop fusion | flops 31457280 | bytes 62963712 | tf_op jit(solution)/shard_map/while/body/eval_jaxpr/convert_element_type | solution.py:103
  1136.6 21.5 %multiply_convert_fusion.8 = bf16[12,512,1024]{2,1,0:T(8,128)(2,1)} fusion(f32[12,512,1024]{2,1,0:T(8,128)} %get-tuple-element.703, f32[12,512,1024]{2,1,0:T(8,128)} %fusion.350, f32[12,512]{1,0:T(8,128)S(1)} %get-tuple-element.704, f32[12,512]{1,0:T(8,128)S(1)} %dynamic-slice_bitcast_fusion.4), kind=kLoop, calls=%fused_computation.32.clone.1 | loop fusion | flops 31457280 | bytes 62963712 | tf_op jit(solution)/shard_map/while/body/eval_jaxpr/convert_element_type | solution.py:103
  1255.7 170.1 %while.57 = (s32[]{:T(128)}, f32[1,1024,12,64]{1,3,2,0:T(8,128)}, f32[1,1024,12,64]{1,3,2,0:T(8,128)}, bf16[2,1,512,12,64]{2,4,3,1,0:T(8,128)(2,1)}, s32[2]{0:T(...) while((s32[]{:T(128)}, f32[1,1024,12,64]{1,3,2,0:T(8,128)}, ...), condition=%wide.region_46.47_spmd.clone, body=%wide.region_44.46_spmd.clone.sunk | while | flops 4106348544 | bytes 217235760 | solution.py:124
  1471.2 46.9 %all-reduce = (f32[768]{0:T(1024)}, f32[768]{0:T(1024)}, f32[768,16]{0,1:T(8,128)}, f32[16,16]{0,1:T(8,128)S(1)}) all-reduce(f32[768]{0:T(1024)S(1)} %add.254, f32[768]{0:T(1024)S(1)} %add.257, f32[768,16]{0,1:T(8,128)S(1)} %copy-done.79, f32[16,16]{0,1:T(8,128)S(1)} %copy-done.134), channel_id=1, replica_groups=mesh['wide'=16,'narrow'=2] {'wide','narrow'}, use_global_device_ids=true, to_apply=%region_51.52 | all-reduce | flops 14080 | bytes 112640 | tf_op jit(solution)/shard_map/psum | solution.py:267
  1526.7 111.5 %all-reduce.4.cloned.1.call-done = (f32[768,2304]{1,0:T(8,128)}, f32[768,768]{1,0:T(8,128)}) async-done(((f32[768,2304]{1,0:T(8,128)}, f32[768,768]{1,0:T(8,128)}), (f32[768,2304]{1,0:T(8,128)}, f32[768,768]{1,0:T(8,128)})) %all-reduce.4.cloned.1.call-update) | async-done | bytes 9437200 | tf_op jit(solution)/shard_map/psum | solution.py:267
  (586 shorter events, 817.5 us)
Async XLA Ops:
  7.2 319.7 %copy-start = (bf16[1,768,1536]{2,1,0:T(8,128)(2,1)S(1)}, bf16[1,768,1536]{2,1,0:T(8,128)(2,1)}, u32[]{:S(2)}) copy-start(bf16[1,768,1536]{2,1,0:T(8,128)(2,1)} %param.36) | copy-start | bytes 7077892
  7.2 319.7 %all-gather.5.cloned.1.call-start = ((), (), s32[]{:S(2)}) async-start(), calls=%async_computation.12 | async-start | bytes 4718592 | tf_op jit(solution)/shard_map/all_gather | solution.py:198
  281.4 131.8 %reduce-scatter.5.cloned.1.call-start = ((), (), s32[]{:S(2)}) async-start(), calls=%async_computation.13 | async-start | bytes 4718592 | tf_op jit(solution)/shard_map/reduce_scatter | solution.py:202
  413.2 37.6 %all-to-all-start.1 = ((bf16[16,64,768]{2,1,0:T(8,128)(2,1)}), bf16[16,64,768]{2,1,0:T(8,128)(2,1)}, u32[]{:S(2)}, u32[]{:S(2)}) async-start(bf16[16,64,768]{2,1,0:T(8,128)(2,1)} %bitcast.472), calls=%async_computation.2 | async-start | bytes 3145728 | tf_op jit(solution)/shard_map/all_to_all | solution.py:205
  418.9 129.3 %all-gather.9.cloned.1.call-start = ((), (), s32[]{:S(2)}) async-start(), calls=%async_computation.16 | async-start | bytes 4718592 | tf_op jit(solution)/shard_map/all_gather | solution.py:228
  419.0 435.0 %copy-start.80 = (f32[16,16]{0,1:T(8,128)}, f32[16,16]{0,1:T(8,128)S(1)}, u32[]{:S(2)}) copy-start(f32[16,16]{0,1:T(8,128)S(1)} %copy.56) | copy-start | bytes 3076
  425.5 428.5 %copy-start.150 = (f32[16]{0:T(128)}, f32[16]{0:T(128)S(1)}, u32[]{:S(2)}) copy-start(f32[16]{0:T(128)S(1)} %add_rsqrt_fusion.2) | copy-start | bytes 196
  427.2 472.5 %copy-start.62 = (f32[1024,16]{0,1:T(8,128)}, f32[1024,16]{0,1:T(8,128)S(1)}, u32[]{:S(2)}) copy-start(f32[1024,16]{0,1:T(8,128)S(1)} %get-tuple-element.465) | copy-start | bytes 196612
  427.2 472.5 %copy-start.90 = (f32[1024]{0:T(1024)}, f32[1024]{0:T(1024)S(1)}, u32[]{:S(2)}) copy-start(f32[1024]{0:T(1024)S(1)} %add_rsqrt_fusion.1) | copy-start | bytes 12292
  427.5 195.5 %copy-start.68 = (f32[1024,16]{0,1:T(8,128)}, f32[1024,16]{0,1:T(8,128)S(1)}, u32[]{:S(2)}) copy-start(f32[1024,16]{0,1:T(8,128)S(1)} %get-tuple-element.467) | copy-start | bytes 196612
  427.5 195.5 %copy-start.110 = (f32[1024]{0:T(1024)}, f32[1024]{0:T(1024)S(1)}, u32[]{:S(2)}) copy-start(f32[1024]{0:T(1024)S(1)} %get-tuple-element.466) | copy-start | bytes 12292
  427.6 195.4 %copy-start.114 = (f32[1024]{0:T(1024)}, f32[1024]{0:T(1024)S(1)}, u32[]{:S(2)}) copy-start(f32[1024]{0:T(1024)S(1)} %fusion.213) | copy-start | bytes 12292
  456.5 166.6 %copy-start.152 = (f32[1024]{0:T(1024)}, f32[1024]{0:T(1024)S(1)}, u32[]{:S(2)}) copy-start(f32[1024]{0:T(1024)S(1)} %get-tuple-element.468) | copy-start | bytes 12292
  503.6 113.7 %reduce-scatter.9.cloned.1.call-start = ((), (), s32[]{:S(2)}) async-start(), calls=%async_computation.17 | async-start | bytes 4718592 | tf_op jit(solution)/shard_map/reduce_scatter | solution.py:234
  617.3 37.6 %all-to-all-start.5 = ((bf16[16,64,768]{2,1,0:T(8,128)(2,1)}), bf16[16,64,768]{2,1,0:T(8,128)(2,1)}, u32[]{:S(2)}, u32[]{:S(2)}) async-start(bf16[16,64,768]{2,1,0:T(8,128)(2,1)} %bitcast.476), calls=%async_computation.8 | async-start | bytes 3145728 | tf_op jit(solution)/shard_map/all_to_all | solution.py:237
  622.9 134.2 %all-gather.7.cloned.1.call-start = ((), (), s32[]{:S(2)}) async-start(), calls=%async_computation.14 | async-start | bytes 4718592 | tf_op jit(solution)/shard_map/all_gather | solution.py:198
  712.6 130.7 %reduce-scatter.7.cloned.1.call-start = ((), (), s32[]{:S(2)}) async-start(), calls=%async_computation.15 | async-start | bytes 4718592 | tf_op jit(solution)/shard_map/reduce_scatter | solution.py:202
  843.3 37.6 %all-to-all-start.3 = ((bf16[16,64,768]{2,1,0:T(8,128)(2,1)}), bf16[16,64,768]{2,1,0:T(8,128)(2,1)}, u32[]{:S(2)}, u32[]{:S(2)}) async-start(bf16[16,64,768]{2,1,0:T(8,128)(2,1)} %bitcast.475), calls=%async_computation.5 | async-start | bytes 3145728 | tf_op jit(solution)/shard_map/all_to_all | solution.py:205
  890.5 41.1 %all-to-all-start.6 = ((bf16[16,64,768]{2,1,0:T(8,128)(2,1)}), bf16[16,64,768]{2,1,0:T(8,128)(2,1)}, u32[]{:S(2)}, u32[]{:S(2)}) async-start(bf16[16,64,768]{2,1,0:T(8,128)(2,1)} %bitcast.477), calls=%async_computation.9 | async-start | bytes 3145728 | tf_op jit(solution)/shard_map/all_to_all | solution.py:225
  899.6 80.5 %all-gather.11.cloned.1.call-start = ((), (), s32[]{:S(2)}) async-start(), calls=%async_computation.18 | async-start | bytes 4718592 | tf_op jit(solution)/shard_map/all_gather | solution.py:228
  931.6 268.7 %reduce-scatter.11.cloned.1.call-start = ((), (), s32[]{:S(2)}) async-start(), calls=%async_computation.19 | async-start | bytes 4718592 | tf_op jit(solution)/shard_map/reduce_scatter | solution.py:234
  1200.3 37.6 %all-to-all-start.7 = ((bf16[16,64,768]{2,1,0:T(8,128)(2,1)}), bf16[16,64,768]{2,1,0:T(8,128)(2,1)}, u32[]{:S(2)}, u32[]{:S(2)}) async-start(bf16[16,64,768]{2,1,0:T(8,128)(2,1)} %bitcast.471), calls=%async_computation.11 | async-start | bytes 3145728 | tf_op jit(solution)/shard_map/all_to_all | solution.py:237
  1206.0 432.2 %all-reduce.4.cloned.1.call-start = ((), (), s32[]{:S(2)}) async-start(), calls=%async_computation.20 | async-start | bytes 18874368 | tf_op jit(solution)/shard_map/psum | solution.py:267
  1466.4 52.4 %copy-start.35 = (bf16[1,1024,768]{1,2,0:T(8,128)(2,1)S(1)}, bf16[1,1024,768]{1,2,0:T(8,128)(2,1)}, u32[]{:S(2)}) copy-start(bf16[1,1024,768]{1,2,0:T(8,128)(2,1)} %get-tuple-element.448) | copy-start | bytes 4718596
  (174 other events, 1089.7 us)
Sparse Core Ops, SparseCore 0:
  281.5 45.3 all-gather.4
  369.7 43.4 reduce-scatter.4
  503.7 44.3 all-gather.8
  573.8 43.4 reduce-scatter.8
  712.7 44.3 all-gather.6
  799.9 43.3 reduce-scatter.6
  931.7 48.4 all-gather.10
  1005.5 43.4 reduce-scatter.10
  1442.5 195.6 all-reduce.3
where the time goes:
time: 1660 us; the launch traced here: 1650 us
  matrix products  599 us (36%)
  waiting for transfers between devices  528 us (32%)
  blocking collectives  180 us (11%)
  other arithmetic  169 us (10%)
  local copies, waits for them, and re-layouts  110 us (7%)
  starting transfers between devices  32.2 us (2%)
  loops' own time  19 us (1%)
    psum x1, waiting for transfers between devices, local(): lax.psum((acc_gain_one, acc_qkv, acc_wo, acc_gain_two, acc_route, acc_emb...  111 us
    dot_general x8, matrix products, one_block(): jnp.einsum('sqhd,skhd->shqk', query_block, keys_in, preferred_element_typ...  101 us
    all_gather x2, waiting for transfers between devices, local(): all_rows = lax.all_gather(arrived, 'narrow', axis=0, tiled=True)  90 us
    all_to_all x2, blocking collectives, local(): lax.all_to_all(sent_rows, 'wide', split_axis=0, concat_axis=0, tiled=True)  88.1 us
    reduce_scatter x2, waiting for transfers between devices, local(): lax.psum_scatter(partial_rows.astype(jnp.bfloat16), 'narrow', scatter_dim...  87.2 us
    convert_element_type x4, other arithmetic, one_block(): grad_scores = (soft_weights * (grad_soft - inner_term)).astype(jnp.bfloat16)  86.1 us
    dot_general x14, matrix products, contract_rows(): lax.dot_general(left, right, (((0,), (0,)), ((), ())), precision=precise,...  76.1 us
    all_gather x2, waiting for transfers between devices, local(): grad_all = lax.all_gather(grad_result, 'narrow', axis=0, tiled=True)  68.2 us
  transfers between devices with their start and end apart: 14, of which 13 were waited for; matrix products, arithmetic and copies ran while one was open for 17% of the time, Pallas kernels for 0%

commit v1 on v0

v1 whole, which is shorter than its diff:
```python
import jax
import jax.numpy as jnp
from jax import lax
from jax.experimental import pallas as pl
from jax.experimental.pallas import tpu as pltpu
from jax.sharding import PartitionSpec as P

D = 768
HEADS = 12
HEAD_DIM = 64
LENGTH = 1024
PAIRS = HEADS // 2
F32 = jnp.float32
BF16 = jnp.bfloat16


def nt(left, right, precision=None):
    return lax.dot_general(
        left, right, (((1,), (1,)), ((), ())), precision=precision, preferred_element_type=F32
    )


def tn(left, right):
    return lax.dot_general(left, right, (((0,), (0,)), ((), ())), preferred_element_type=F32)


def attend_forward_kernel(q_ref, k_ref, v_ref, out_ref, stat_ref):
    rows = q_ref.shape[0]
    low_half = lax.broadcasted_iota(jnp.int32, (rows, 128), 1) < HEAD_DIM
    queries = q_ref[...] * jnp.asarray(HEAD_DIM**-0.5, BF16)
    keys = k_ref[...]
    values = v_ref[...]
    zero = jnp.zeros_like(keys)
    one = jnp.ones_like(keys)
    mixed = []
    logs = []
    for half in range(2):
        mine = low_half if half == 0 else jnp.logical_not(low_half)
        scores = nt(queries, jnp.where(mine, keys, zero))
        row_max = jnp.max(scores, axis=-1, keepdims=True)
        weights = jnp.exp(scores - row_max).astype(BF16)
        both = jnp.dot(weights, jnp.where(mine, values, one), preferred_element_type=F32)
        total = pltpu.roll(both, HEAD_DIM, 1)
        mixed.append(both / total)
        logs.append(row_max + jnp.log(both))
    out_ref[...] = jnp.where(low_half, mixed[0], mixed[1]).astype(BF16)
    stats = jnp.where(low_half, logs[1], logs[0]).T
    stat_ref[0:8, :] = stats[HEAD_DIM : HEAD_DIM + 8]
    stat_ref[8:16, :] = stats[0:8]


def attend_forward(qkv_rows):
    count = qkv_rows.shape[0]
    seqs = count // LENGTH
    spec = lambda off: pl.BlockSpec((LENGTH, 128), lambda s, j, off=off: (s, off + j))
    return pl.pallas_call(
        attend_forward_kernel,
        grid=(seqs, PAIRS),
        in_specs=[spec(0), spec(PAIRS), spec(2 * PAIRS)],
        out_specs=[
            spec(0),
            pl.BlockSpec((None, None, 16, LENGTH), lambda s, j: (s, j, 0, 0)),
        ],
        out_shape=[
            jax.ShapeDtypeStruct((count, D), BF16),
            jax.ShapeDtypeStruct((seqs, PAIRS, 16, LENGTH), F32),
        ],
        compiler_params=pltpu.CompilerParams(vmem_limit_bytes=56 << 20),
        cost_estimate=pl.CostEstimate(
            flops=seqs * HEADS * 8 * LENGTH * LENGTH * HEAD_DIM,
            bytes_accessed=count * D * 8,
            transcendentals=seqs * HEADS * LENGTH * LENGTH,
        ),
        name="attend_forward",
    )(qkv_rows, qkv_rows, qkv_rows)


def attend_backward_kernel(q_ref, k_ref, v_ref, o_ref, g_ref, stat_ref, gq_ref, gk_ref, gv_ref):
    rows = q_ref.shape[0]
    scale = HEAD_DIM**-0.5
    low_half = lax.broadcasted_iota(jnp.int32, (rows, 128), 1) < HEAD_DIM
    queries = q_ref[...] * jnp.asarray(scale, BF16)
    keys = k_ref[...]
    values = v_ref[...]
    grads = g_ref[...]
    zero = jnp.zeros_like(keys)
    picker = (
        (lax.broadcasted_iota(jnp.int32, (16, 128), 1) >= HEAD_DIM)
        == (lax.broadcasted_iota(jnp.int32, (16, 128), 0) >= 8)
    ).astype(F32)
    inner = nt(picker, grads.astype(F32) * o_ref[...].astype(F32), lax.Precision.HIGHEST)
    grad_q = []
    grad_k = []
    grad_v = []
    for half in range(2):
        mine = low_half if half == 0 else jnp.logical_not(low_half)
        at = 8 * half
        keys_half = jnp.where(mine, keys, zero)
        weights = jnp.exp(nt(keys_half, queries) - stat_ref[at : at + 1, :])
        grad_soft = nt(jnp.where(mine, values, zero), grads)
        grad_scores = (weights * (grad_soft - inner[at : at + 1, :])).astype(BF16)
        grad_v.append(jnp.dot(weights.astype(BF16), grads, preferred_element_type=F32))
        grad_k.append(jnp.dot(grad_scores, queries, preferred_element_type=F32))
        grad_q.append(tn(grad_scores, keys_half))
    gq_ref[...] = ((grad_q[0] + grad_q[1]) * scale).astype(BF16)
    gk_ref[...] = jnp.where(low_half, grad_k[0], grad_k[1]).astype(BF16)
    gv_ref[...] = jnp.where(low_half, grad_v[0], grad_v[1]).astype(BF16)


def attend_backward(qkv_rows, mixed_rows, grad_mixed, stats):
    count = qkv_rows.shape[0]
    seqs = count // LENGTH
    spec = lambda off: pl.BlockSpec((LENGTH, 128), lambda s, j, off=off: (s, off + j))
    return pl.pallas_call(
        attend_backward_kernel,
        grid=(seqs, PAIRS),
        in_specs=[spec(0), spec(PAIRS), spec(2 * PAIRS), spec(0), spec(0),
            pl.BlockSpec((None, None, 16, LENGTH), lambda s, j: (s, j, 0, 0)),
        ],
        out_specs=[spec(0), spec(0), spec(0)],
        out_shape=[jax.ShapeDtypeStruct((count, D), BF16)] * 3,
        compiler_params=pltpu.CompilerParams(vmem_limit_bytes=56 << 20),
        cost_estimate=pl.CostEstimate(
            flops=seqs * HEADS * 20 * LENGTH * LENGTH * HEAD_DIM,
            bytes_accessed=count * D * 16,
            transcendentals=seqs * HEADS * LENGTH * LENGTH,
        ),
        name="attend_backward",
    )(qkv_rows, qkv_rows, qkv_rows, mixed_rows, grad_mixed, stats)


def layer_norm(values, gain_vec):
    centred = values - jnp.mean(values, axis=-1, keepdims=True)
    spread_sq = jnp.mean(centred * centred, axis=-1, keepdims=True)
    return centred * lax.rsqrt(spread_sq + 1e-05) * gain_vec


def gate_from(projected, embed_rows, route_row):
    unit_rows = projected * lax.rsqrt(jnp.sum(projected * projected, axis=-1, keepdims=True) + 1.0)
    anchor = embed_rows * lax.rsqrt(jnp.sum(embed_rows * embed_rows, axis=-1, keepdims=True) + 1.0)
    logits = 3.0 * jnp.dot(
        unit_rows, anchor.T, precision=lax.Precision.HIGHEST, preferred_element_type=F32
    )
    soft_rows = jax.nn.softmax(logits, axis=-1)
    picked = route_row[:, None] == jnp.arange(soft_rows.shape[1], dtype=jnp.int32)[None, :]
    return jnp.sum(jnp.where(picked, soft_rows, 0.0), axis=-1)


def contract_rows(left, right, precise=None):
    return lax.dot_general(
        left, right, (((0,), (0,)), ((), ())), precision=precise, preferred_element_type=F32
    )


def shifted(value, axis, step):
    count = lax.axis_size(axis)
    return lax.ppermute(value, axis, [(src, (src + step) % count) for src in range(count)])


def exchange(rows):
    return lax.all_to_all(rows, "wide", split_axis=0, concat_axis=0, tiled=True)


def gelu_parts(pre):
    cdf = 0.5 * (1.0 + lax.erf(pre * 0.7071067811865476))
    return pre * cdf, cdf + pre * jnp.exp(-0.5 * pre * pre) * 0.3989422804014327


def expert_pass(rows, grads, parts_in, parts_outer):
    result = 0.0
    grad_rows = 0.0
    terms_in = []
    terms_outer = []
    for first, second in zip(parts_in, parts_outer):
        pre = jnp.dot(rows, first, preferred_element_type=F32)
        hidden, slope = gelu_parts(pre)
        hidden = hidden.astype(BF16)
        result = result + jnp.dot(hidden, second, preferred_element_type=F32)
        grad_pre = (nt(grads, second) * slope).astype(BF16)
        terms_outer.append(contract_rows(hidden, grads))
        terms_in.append(contract_rows(rows, grad_pre))
        grad_rows = grad_rows + nt(grad_pre, first)
    return result.astype(BF16), grad_rows.astype(BF16), terms_in, terms_outer


def local(
    tokens,
    grad_out,
    route_ids,
    slot_ids,
    keep_ids,
    gain_one,
    w_query,
    w_key,
    w_value,
    w_out,
    gain_two,
    w_route,
    embed,
    w_in,
    w_outer,
):
    micro_count, tok_count, width = tokens.shape
    narrow_count = lax.axis_size("narrow")
    expert_count = embed.shape[0]
    slot_cap = max(2, tok_count // expert_count)
    w_qkv = jnp.concatenate([w_query, w_key, w_value], axis=1)
    route_float = w_route.astype(F32)
    slot_columns = jnp.arange(expert_count * slot_cap, dtype=jnp.int32)
    parts_in = [w_in[0]] + [shifted(w_in[0], "narrow", k) for k in range(1, narrow_count)]
    parts_outer = [w_outer[0]] + [shifted(w_outer[0], "narrow", k) for k in range(1, narrow_count)]

    def before(step):
        inputs = tokens[step].astype(F32)
        normed_one, pull_one = jax.vjp(layer_norm, inputs, gain_one)
        normed_low = normed_one.astype(BF16)
        qkv = jnp.dot(normed_low, w_qkv, preferred_element_type=F32).astype(BF16)
        mixed, stats = attend_forward(qkv)
        first_sum = inputs + jnp.dot(mixed, w_out, preferred_element_type=F32)
        normed_two, pull_two = jax.vjp(layer_norm, first_sum, gain_two)
        second_low = normed_two.astype(BF16)
        projected = jnp.dot(second_low, w_route, preferred_element_type=F32)
        gate, pull_gate = jax.vjp(
            lambda proj_in, embed_in: gate_from(proj_in, embed_in, route_ids[step]),
            projected,
            embed,
        )
        slot_index = jnp.where(
            keep_ids[step] > 0, route_ids[step] * slot_cap + slot_ids[step], -1
        )
        table = (slot_index[:, None] == slot_columns[None, :]).astype(BF16)
        grad_sum = grad_out[step].astype(F32)
        sent = contract_rows(table, second_low).astype(BF16)
        arrived = exchange(sent.reshape(expert_count, slot_cap, width)).reshape(-1, width)
        grad_low = (gate[:, None] * grad_sum).astype(BF16)
        grad_buffer = contract_rows(table, grad_low).astype(BF16)
        grad_all = exchange(grad_buffer.reshape(expert_count, slot_cap, width)).reshape(-1, width)
        keep = dict(
            pull_one=pull_one, normed_low=normed_low, qkv=qkv, mixed=mixed, stats=stats,
            first_sum=first_sum, pull_two=pull_two, second_low=second_low, gate=gate,
            pull_gate=pull_gate, table=table, grad_sum=grad_sum,
        )
        return keep, arrived, grad_all

    def home(rows):
        return exchange(rows.reshape(-1, slot_cap, width)).reshape(-1, width)

    def after(kept, back_rows, back_grads):
        returned = jnp.dot(kept["table"], back_rows, preferred_element_type=F32)
        grad_sum = kept["grad_sum"]
        out = (kept["first_sum"] + kept["gate"][:, None] * returned).astype(BF16)
        grad_gate = jnp.sum(grad_sum * returned, axis=-1)
        grad_second = jnp.dot(kept["table"], back_grads, preferred_element_type=F32)
        grad_projected, term_embed = kept["pull_gate"](grad_gate)
        grad_second = grad_second + nt(grad_projected, route_float, lax.Precision.HIGHEST)
        term_route = contract_rows(
            kept["second_low"].astype(F32), grad_projected, lax.Precision.HIGHEST
        )
        grad_first_norm, term_gain_two = kept["pull_two"](grad_second)
        grad_first = grad_sum + grad_first_norm
        grad_branch = grad_first.astype(BF16)
        term_wo = contract_rows(kept["mixed"], grad_branch)
        grad_mixed = nt(grad_branch, w_out).astype(BF16)
        grad_heads = attend_backward(kept["qkv"], kept["mixed"], grad_mixed, kept["stats"])
        terms = [contract_rows(kept["normed_low"], part) for part in grad_heads]
        grad_normed = sum(
            nt(part, weight) for part, weight in zip(grad_heads, (w_query, w_key, w_value))
        )
        grad_input_norm, term_gain_one = kept["pull_one"](grad_normed)
        grad_input = (grad_first + grad_input_norm).astype(BF16)
        return out, grad_input, terms + [term_wo], [term_gain_one, term_gain_two, term_route, term_embed]

    add = lambda left, right: jax.tree.map(jnp.add, left, right)
    everywhere = ("wide", "narrow")
    fronts = [before(step) for step in range(micro_count)]
    terms_in = terms_outer = None
    homes = []
    for kept, arrived, grad_all in fronts:
        result, grad_rows, more_in, more_outer = expert_pass(arrived, grad_all, parts_in, parts_outer)
        homes.append((home(result), home(grad_rows)))
        terms_in = more_in if terms_in is None else add(terms_in, more_in)
        terms_outer = more_outer if terms_outer is None else add(terms_outer, more_outer)
    sum_in, sum_outer = terms_in[0], terms_outer[0]
    for k in range(1, narrow_count):
        sum_in = sum_in + shifted(terms_in[k].astype(BF16), "narrow", -k).astype(F32)
        sum_outer = sum_outer + shifted(terms_outer[k].astype(BF16), "narrow", -k).astype(F32)
    outputs = []
    input_grads = []
    large = small = None
    for (kept, _, _), (back_rows, back_grads) in zip(fronts, homes):
        out, grad_input, more_large, more_small = after(kept, back_rows, back_grads)
        outputs.append(out)
        input_grads.append(grad_input)
        large = more_large if large is None else add(large, more_large)
        small = more_small if small is None else add(small, more_small)
    large = [reduce_large(item) for item in large]
    small = lax.psum(small, everywhere)
    return (
        jnp.stack(outputs),
        jnp.stack(input_grads),
        small[0],
        large[0],
        large[1],
        large[2],
        large[3],
        small[1],
        small[2],
        small[3],
        sum_in[None],
        sum_outer[None],
    )


def reduce_large(item):
    return lax.psum(item.astype(BF16), ("wide", "narrow")).astype(F32)


def solution(mesh):
    placed = (
        P(None, ("wide", "narrow"), None),
        P(None, ("wide", "narrow"), None),
        P(None, ("wide", "narrow")),
        P(None, ("wide", "narrow")),
        P(None, ("wide", "narrow")),
        P(),
        P(),
        P(),
        P(),
        P(),
        P(),
        P(),
        P(),
        P("wide", None, "narrow"),
        P("wide", "narrow", None),
    )
    return jax.shard_map(
        local,
        mesh=mesh,
        in_specs=placed,
        out_specs=(
            P(None, ("wide", "narrow"), None),
            P(None, ("wide", "narrow"), None),
            P(),
            P(),
            P(),
            P(),
            P(),
            P(),
            P(),
            P(),
            P("wide", None, "narrow"),
            P("wide", "narrow", None),
        ),
        check_vma=False,
    )
```

time: 1660 us -> 950 us (0.57)
  matrix products: 599 us -> 256 us
  waiting for transfers between devices: 528 us -> 311 us
  Pallas kernels: 0 us -> 137 us
  other arithmetic: 169 us -> 37 us
  blocking collectives: 180 us -> 91.2 us
  local copies, waits for them, and re-layouts: 110 us -> 34.9 us
  starting transfers between devices: 32.2 us -> 57.6 us
  loops' own time: 19 us -> 0 us
    dot_general x52 -> x36, matrix products: 521 us -> 167 us  [the longest x18 85 us: nt(): lax.dot_general(left, right, (((1,), (1,)), ((), ())), precision=precisio...]
    all_gather x4 -> x0, waiting for transfers between devices: 158 us -> none  [the longest x2 90 us: local(): all_rows = lax.all_gather(arrived, 'narrow', axis=0, tiled=True)]
    pallas_call x0 -> x4, Pallas kernels: none -> 137 us  [the longest x2 88.9 us: attend_backward(): pl.pallas_call(attend_backward_kernel, grid=(seqs, PAIRS), in_specs=[spec...]
    reduce_scatter x4 -> x0, waiting for transfers between devices: 131 us -> none  [the longest x2 87.2 us: local(): lax.psum_scatter(partial_rows.astype(jnp.bfloat16), 'narrow', scatter_dim...]
    ppermute x0 -> x4, waiting for transfers between devices: none -> 124 us  [shifted(): lax.ppermute(value, axis, [(src, (src + step) % count) for src in range(c...]
    all_to_all x3 -> x1, blocking collectives: 133 us -> 45.3 us  [exchange(): return lax.all_to_all(rows, 'wide', split_axis=0, concat_axis=0, tiled=True)]
    convert_element_type x7, other arithmetic: 87.7 us -> 13.5 us  [the longest x4 7.72 us: reduce_large(): return lax.psum(item.astype(BF16), ('wide', 'narrow')).astype(F32)]
    reduce_sum x4 -> x0, other arithmetic: 44.9 us -> none  [one_block(): row_total = jnp.sum(exp_scores, axis=-1, keepdims=True)]
  transfers between devices with their start and end apart: 14 -> 12, of which waited for: 13 -> 10; matrix products, arithmetic and copies ran while one was open for 17% -> 14% of each run, Pallas kernels for 0% -> 5%
where the time goes in v1:
time: 950 us; the launch traced here: 941 us
  waiting for transfers between devices  311 us (33%)
  matrix products  256 us (27%)
  Pallas kernels  137 us (14%)
  blocking collectives  91.2 us (10%)
  starting transfers between devices  57.6 us (6%)
  other arithmetic  37 us (4%)
  local copies, waits for them, and re-layouts  34.9 us (4%)
  between operations  15.9 us (2%)
    ppermute x4, waiting for transfers between devices, shifted(): lax.ppermute(value, axis, [(src, (src + step) % count) for src in range(c...  124 us
    all_to_all x7, waiting for transfers between devices, exchange(): return lax.all_to_all(rows, 'wide', split_axis=0, concat_axis=0, tiled=True)  102 us
    pallas_call x2, Pallas kernels, attend_backward(): pl.pallas_call(attend_backward_kernel, grid=(seqs, PAIRS), in_specs=[spec...  88.9 us
    dot_general x22, matrix products, contract_rows(): lax.dot_general(left, right, (((0,), (0,)), ((), ())), precision=precise,...  87.5 us
    psum x1, waiting for transfers between devices, reduce_large(): return lax.psum(item.astype(BF16), ('wide', 'narrow')).astype(F32)  85.3 us
    dot_general x18, matrix products, nt(): lax.dot_general(left, right, (((1,), (1,)), ((), ())), precision=precisio...  85 us
    all_to_all x7, starting transfers between devices, exchange(): return lax.all_to_all(rows, 'wide', split_axis=0, concat_axis=0, tiled=True)  53.4 us
    pallas_call x2, Pallas kernels, attend_forward(): pl.pallas_call(attend_forward_kernel, grid=(seqs, PAIRS), in_specs=[spec(...  48.6 us
  transfers between devices with their start and end apart: 12, of which 10 were waited for; matrix products, arithmetic and copies ran while one was open for 14% of the time, Pallas kernels for 5%

profile of v1, /device:TPU:0, one launch (start us, length us, event | category | flops | bytes accessed | tf_op | source)
XLA Modules:
  0.0 941.1 jit_solution(1449343834995972698)
XLA Ops:
  19.2 7.8 convolution_convert_fusion.q_ref.k_ref.v_ref
  26.9 24.1 %attend_forward.3 = (bf16[1024,768]{1,0:T(8,128)(2,1)}, f32[1,6,16,1024]{3,2,1,0:T(8,128)}) custom-call(bf16[1024,2304]{1,0:T(8,128)(2,1)} %convolution_convert_fusion.q_ref.k_ref.v_ref, bf16[1024,2304]{1,0:T(8,128)(2,1)} %convolution_convert_fusion.q_ref.k_ref.v_ref, bf16[1024,2304]{1,0:T(8,128)(2,1)} %convolution_convert_fusion.q_ref.k_ref.v_ref), custom_call_target="tpu_custom_call" | custom-call | flops 6442450944 | bytes 6291456 | tf_op jit(solution)/shard_map/attend_forward/pallas_call | solution.py:56
  62.5 24.4 %attend_forward.2 = (bf16[1024,768]{1,0:T(8,128)(2,1)}, f32[1,6,16,1024]{3,2,1,0:T(8,128)}) custom-call(bf16[1024,2304]{1,0:T(8,128)(2,1)} %convolution_convert_fusion.1.q_ref.k_ref.v_ref, bf16[1024,2304]{1,0:T(8,128)(2,1)} %convolution_convert_fusion.1.q_ref.k_ref.v_ref, bf16[1024,2304]{1,0:T(8,128)(2,1)} %convolution_convert_fusion.1.q_ref.k_ref.v_ref), custom_call_target="tpu_custom_call" | custom-call | flops 6442450944 | bytes 6291456 | tf_op jit(solution)/shard_map/attend_forward/pallas_call | solution.py:56
  95.4 7.8 all-to-all-start
  105.3 29.7 %all-to-all-done = bf16[16,64,768]{2,1,0:T(8,128)(2,1)S(1)} async-done(((bf16[16,64,768]{2,1,0:T(8,128)(2,1)}), bf16[16,64,768]{2,1,0:T(8,128)(2,1)S(1)}, u32[]{:S(2)}, u32[]{:S(2)}) %all-to-all-start) | async-done | bytes 1572896 | tf_op jit(solution)/shard_map/all_to_all | solution.py:161
  141.5 16.2 %collective-permute-done = bf16[768,1536]{1,0:T(8,128)(2,1)} collective-permute-done((bf16[768,1536]{1,0:T(8,128)(2,1)}, bf16[768,1536]{1,0:T(8,128)(2,1)}, u32[]{:S(2)}, u32[]{:S(2)}) %collective-permute-start) | collective-permute-done | bytes 2359328 | tf_op jit(solution)/shard_map/ppermute | solution.py:157
  166.9 40.9 %collective-permute-done.1 = bf16[1536,768]{1,0:T(8,128)(2,1)} collective-permute-done((bf16[1536,768]{1,0:T(8,128)(2,1)}, bf16[1536,768]{1,0:T(8,128)(2,1)}, u32[]{:S(2)}, u32[]{:S(2)}) %collective-permute-start.1) | collective-permute-done | bytes 2359328 | tf_op jit(solution)/shard_map/ppermute | solution.py:157
  227.6 23.2 %all-to-all-done.1 = bf16[16,64,768]{2,1,0:T(8,128)(2,1)} async-done(((bf16[16,64,768]{2,1,0:T(8,128)(2,1)}), bf16[16,64,768]{2,1,0:T(8,128)(2,1)}, u32[]{:S(2)}, u32[]{:S(2)}) %all-to-all-start.1) | async-done | bytes 1572896 | tf_op jit(solution)/shard_map/all_to_all | solution.py:161
  258.7 45.3 %all_to_all.40 = bf16[16,64,768]{2,1,0:T(8,128)(2,1)S(1)} all-to-all(bf16[16,64,768]{2,1,0:T(8,128)(2,1)S(1)} %bitcast.247), channel_id=1, replica_groups=mesh['wide'=16,'narrow'=2] {'wide'}, dimensions={0} | all-to-all | bytes 3145728 | tf_op jit(solution)/shard_map/all_to_all | solution.py:161
  340.7 20.1 %all-to-all-done.5 = bf16[16,64,768]{2,1,0:T(8,128)(2,1)} async-done(((bf16[16,64,768]{2,1,0:T(8,128)(2,1)}), bf16[16,64,768]{2,1,0:T(8,128)(2,1)}, u32[]{:S(2)}, u32[]{:S(2)}) %all-to-all-start.5) | async-done | bytes 1572896 | tf_op jit(solution)/shard_map/all_to_all | solution.py:161
  374.5 9.6 %all-to-all-start.2 = ((bf16[16,64,768]{2,1,0:T(8,128)(2,1)}), bf16[16,64,768]{2,1,0:T(8,128)(2,1)}, u32[]{:S(2)}, u32[]{:S(2)}) async-start(bf16[16,64,768]{2,1,0:T(8,128)(2,1)} %bitcast.242), calls=%async_computation.2 | async-start | bytes 3145728 | tf_op jit(solution)/shard_map/all_to_all | solution.py:161
  399.9 16.0 %all-to-all-done.2 = bf16[16,64,768]{2,1,0:T(8,128)(2,1)} async-done(((bf16[16,64,768]{2,1,0:T(8,128)(2,1)}), bf16[16,64,768]{2,1,0:T(8,128)(2,1)}, u32[]{:S(2)}, u32[]{:S(2)}) %all-to-all-start.2) | async-done | bytes 1572896 | tf_op jit(solution)/shard_map/all_to_all | solution.py:161
  438.2 9.4 %all-to-all-start.3 = ((bf16[16,64,768]{2,1,0:T(8,128)(2,1)}), bf16[16,64,768]{2,1,0:T(8,128)(2,1)}, u32[]{:S(2)}, u32[]{:S(2)}) async-start(bf16[16,64,768]{2,1,0:T(8,128)(2,1)} %bitcast.245), calls=%async_computation.3 | async-start | bytes 3145728 | tf_op jit(solution)/shard_map/all_to_all | solution.py:161
  452.8 44.2 %attend_backward.2 = (bf16[1024,768]{1,0:T(8,128)(2,1)}, bf16[1024,768]{1,0:T(8,128)(2,1)}, bf16[1024,768]{1,0:T(8,128)(2,1)}) custom-call(bf16[1024,2304]{1,0:T(8,128)(2,1)} %convolution_convert_fusion.1.q_ref.k_ref.v_ref, bf16[1024,2304]{1,0:T(8,128)(2,1)} %convolution_convert_fusion.1.q_ref.k_ref.v_ref, ...), custom_call_target="tpu_custom_call" | custom-call | flops 16106127360 | bytes 12582912 | tf_op jit(solution)/shard_map/attend_backward/pallas_call | solution.py:114
  539.0 12.7 %all-to-all-done.6 = bf16[16,64,768]{2,1,0:T(8,128)(2,1)} async-done(((bf16[16,64,768]{2,1,0:T(8,128)(2,1)}), bf16[16,64,768]{2,1,0:T(8,128)(2,1)}, u32[]{:S(2)}, u32[]{:S(2)}) %all-to-all-start.6) | async-done | bytes 1572896 | tf_op jit(solution)/shard_map/all_to_all | solution.py:161
  558.5 7.8 fusion.23
  588.1 9.3 all-to-all-start.7
  600.6 25.7 %collective-permute-done.2 = bf16[768,1536]{1,0:T(8,128)(2,1)} collective-permute-done((bf16[768,1536]{1,0:T(8,128)(2,1)}, bf16[768,1536]{1,0:T(8,128)(2,1)}, u32[]{:S(2)}, u32[]{:S(2)}) %collective-permute-start.2) | collective-permute-done | bytes 2359328 | tf_op jit(solution)/shard_map/ppermute | solution.py:157
  626.4 9.3 add_bitcast_fusion.1
  635.7 41.3 %collective-permute-done.3 = bf16[1536,768]{1,0:T(8,128)(2,1)} collective-permute-done((bf16[1536,768]{1,0:T(8,128)(2,1)}, bf16[1536,768]{1,0:T(8,128)(2,1)}, u32[]{:S(2)}, u32[]{:S(2)}) %collective-permute-start.3) | collective-permute-done | bytes 2359328 | tf_op jit(solution)/shard_map/ppermute | solution.py:157
  704.3 44.7 %attend_backward.3 = (bf16[1024,768]{1,0:T(8,128)(2,1)}, bf16[1024,768]{1,0:T(8,128)(2,1)}, bf16[1024,768]{1,0:T(8,128)(2,1)}) custom-call(bf16[1024,2304]{1,0:T(8,128)(2,1)} %convolution_convert_fusion.q_ref.k_ref.v_ref, bf16[1024,2304]{1,0:T(8,128)(2,1)} %convolution_convert_fusion.q_ref.k_ref.v_ref, ...), custom_call_target="tpu_custom_call" | custom-call | flops 16106127360 | bytes 12582912 | tf_op jit(solution)/shard_map/attend_backward/pallas_call | solution.py:114
  767.0 9.4 fusion.49
  794.2 45.9 %all-reduce = (f32[768]{0:T(1024)}, f32[768]{0:T(1024)}, f32[768,16]{0,1:T(8,128)}, f32[16,16]{0,1:T(8,128)S(1)}) all-reduce(f32[768]{0:T(1024)S(1)} %add.258, f32[768]{0:T(1024)S(1)} %add.263, f32[768,16]{0,1:T(8,128)S(1)} %convolution_add_fusion.2, f32[16,16]{0,1:T(8,128)S(1)} %fusion.123), channel_id=1, replica_groups=mesh['wide'=16,'narrow'=2] {'wide','narrow'}, use_global_device_ids=true, to_apply=%region_33.34 | all-reduce | flops 14080 | bytes 112640 | tf_op jit(solution)/shard_map/psum | solution.py:297
  840.8 85.3 %all-reduce.4.cloned.1.call-done = (bf16[768,768]{1,0:T(8,128)(2,1)}, bf16[768,768]{1,0:T(8,128)(2,1)}, bf16[768,768]{1,0:T(8,128)(2,1)}, bf16[768,768]{1,0:T(8,128)(2,1)}) async-done(((bf16[768,768]{1,0:T(8,128)(2,1)}, bf16[768,768]{1,0:T(8,128)(2,1)}, bf16[768,768]{1,0:T(8,128)(2,1)}, bf16[768,768]{1,0:T(8,128)(2,1)}), (bf16[768,768]{1,0:T(8,128)(2,1)}, bf16[768,768]{1,0:T(8,128)(2,1)}, ...) | async-done | bytes 4718608 | tf_op jit(solution)/shard_map/psum | solution.py:315
  (366 shorter events, 315.1 us)
Async XLA Ops:
  7.2 79.7 %copy-start = (bf16[768,768]{1,0:T(8,128)(2,1)S(1)}, bf16[768,768]{1,0:T(8,128)(2,1)}, u32[]{:S(2)}) copy-start(bf16[768,768]{1,0:T(8,128)(2,1)} %param.24) | copy-start | bytes 3538948
  90.1 277.5 %copy-start.41 = (f32[1024]{0:T(1024)}, f32[1024]{0:T(1024)S(1)}, u32[]{:S(2)}) copy-start(f32[1024]{0:T(1024)S(1)} %broadcast_multiply_fusion) | copy-start | bytes 12292
  91.1 276.5 %copy-start.49 = (f32[1024]{0:T(1024)}, f32[1024]{0:T(1024)S(1)}, u32[]{:S(2)}) copy-start(f32[1024]{0:T(1024)S(1)} %get-tuple-element.125) | copy-start | bytes 12292
  95.4 39.6 %all-to-all-start = ((bf16[16,64,768]{2,1,0:T(8,128)(2,1)}), bf16[16,64,768]{2,1,0:T(8,128)(2,1)S(1)}, u32[]{:S(2)}, u32[]{:S(2)}) async-start(bf16[16,64,768]{2,1,0:T(8,128)(2,1)} %bitcast.246), calls=%async_computation | async-start | bytes 3145728 | tf_op jit(solution)/shard_map/all_to_all | solution.py:161
  103.2 54.5 %collective-permute-start = (bf16[768,1536]{1,0:T(8,128)(2,1)}, bf16[768,1536]{1,0:T(8,128)(2,1)}, u32[]{:S(2)}, u32[]{:S(2)}) collective-permute-start(bf16[768,1536]{1,0:T(8,128)(2,1)} %bitcast.259), channel_id=1, source_target_pairs={{0,1},{1,0},{2,3},{3,2},{4,5},{5,4},{6,7},{7,6},{8,9},{9,8},{10,11... | collective-permute-start | bytes 7077896 | tf_op jit(solution)/shard_map/ppermute | solution.py:157
  104.8 103.0 %collective-permute-start.1 = (bf16[1536,768]{1,0:T(8,128)(2,1)}, bf16[1536,768]{1,0:T(8,128)(2,1)}, u32[]{:S(2)}, u32[]{:S(2)}) collective-permute-start(bf16[1536,768]{1,0:T(8,128)(2,1)} %bitcast.258), channel_id=1, source_target_pairs={{0,1},{1,0},{2,3},{3,2},{4,5},{5,4},{6,7},{7,6},{8,9},{9,8},{10,11... | collective-permute-start | bytes 7077896 | tf_op jit(solution)/shard_map/ppermute | solution.py:157
  213.1 37.7 %all-to-all-start.1 = ((bf16[16,64,768]{2,1,0:T(8,128)(2,1)}), bf16[16,64,768]{2,1,0:T(8,128)(2,1)}, u32[]{:S(2)}, u32[]{:S(2)}) async-start(bf16[16,64,768]{2,1,0:T(8,128)(2,1)} %bitcast.243), calls=%async_computation.1 | async-start | bytes 3145728 | tf_op jit(solution)/shard_map/all_to_all | solution.py:161
  250.8 53.1 %slice-start.2 = ((s8[6291456]{0:T(1024)(128)(4,1)}), s8[4194304]{0:T(1024)(128)(4,1)S(1)}, s32[]{:S(2)}) async-start(s8[6291456]{0:T(1024)(128)(4,1)} %bitcast.260), calls=%async_computation.11 | async-start | bytes 8388608
  256.6 47.4 %slice-start.3 = ((s8[6291456]{0:T(1024)(128)(4,1)}), s8[2097152]{0:T(1024)(128)(4,1)S(1)}, s32[]{:S(2)}) async-start(s8[6291456]{0:T(1024)(128)(4,1)} %bitcast.260), calls=%async_computation.12 | async-start | bytes 4194304
  258.7 45.3 %copy-start.73 = (bf16[1,1536,768]{2,1,0:T(8,128)(2,1)S(1)}, bf16[1,1536,768]{2,1,0:T(8,128)(2,1)}, u32[]{:S(2)}) copy-start(bf16[1,1536,768]{2,1,0:T(8,128)(2,1)} %param.29) | copy-start | bytes 7077892
  258.7 53.2 %slice-start.4 = ((s8[6291456]{0:T(1024)(128)(4,1)}), s8[4194304]{0:T(1024)(128)(4,1)S(1)}, s32[]{:S(2)}) async-start(s8[6291456]{0:T(1024)(128)(4,1)} %bitcast.262), calls=%async_computation.13 | async-start | bytes 8388608
  323.8 37.0 %all-to-all-start.5 = ((bf16[16,64,768]{2,1,0:T(8,128)(2,1)}), bf16[16,64,768]{2,1,0:T(8,128)(2,1)}, u32[]{:S(2)}, u32[]{:S(2)}) async-start(bf16[16,64,768]{2,1,0:T(8,128)(2,1)} %bitcast.244), calls=%async_computation.5 | async-start | bytes 3145728 | tf_op jit(solution)/shard_map/all_to_all | solution.py:161
  374.5 41.5 %all-to-all-start.2 = ((bf16[16,64,768]{2,1,0:T(8,128)(2,1)}), bf16[16,64,768]{2,1,0:T(8,128)(2,1)}, u32[]{:S(2)}, u32[]{:S(2)}) async-start(bf16[16,64,768]{2,1,0:T(8,128)(2,1)} %bitcast.242), calls=%async_computation.2 | async-start | bytes 3145728 | tf_op jit(solution)/shard_map/all_to_all | solution.py:161
  399.9 47.8 %copy-start.61 = (f32[1024]{0:T(1024)}, f32[1024]{0:T(1024)S(1)}, u32[]{:S(2)}) copy-start(f32[1024]{0:T(1024)S(1)} %negate_multiply_fusion.3) | copy-start | bytes 12292
  438.2 66.5 %all-to-all-start.3 = ((bf16[16,64,768]{2,1,0:T(8,128)(2,1)}), bf16[16,64,768]{2,1,0:T(8,128)(2,1)}, u32[]{:S(2)}, u32[]{:S(2)}) async-start(bf16[16,64,768]{2,1,0:T(8,128)(2,1)} %bitcast.245), calls=%async_computation.3 | async-start | bytes 3145728 | tf_op jit(solution)/shard_map/all_to_all | solution.py:161
  513.2 38.4 %all-to-all-start.6 = ((bf16[16,64,768]{2,1,0:T(8,128)(2,1)}), bf16[16,64,768]{2,1,0:T(8,128)(2,1)}, u32[]{:S(2)}, u32[]{:S(2)}) async-start(bf16[16,64,768]{2,1,0:T(8,128)(2,1)} %bitcast.241), calls=%async_computation.6 | async-start | bytes 3145728 | tf_op jit(solution)/shard_map/all_to_all | solution.py:161
  571.9 54.4 %collective-permute-start.2 = (bf16[768,1536]{1,0:T(8,128)(2,1)}, bf16[768,1536]{1,0:T(8,128)(2,1)}, u32[]{:S(2)}, u32[]{:S(2)}) collective-permute-start(bf16[768,1536]{1,0:T(8,128)(2,1)} %add_convert_fusion.1), channel_id=1, source_target_pairs={{0,1},{1,0},{2,3},{3,2},{4,5},{5,4},{6,7},{7,6},{8,9},{9,8},{10,11... | collective-permute-start | bytes 7077896 | tf_op jit(solution)/shard_map/ppermute | solution.py:157
  579.4 97.5 %collective-permute-start.3 = (bf16[1536,768]{1,0:T(8,128)(2,1)}, bf16[1536,768]{1,0:T(8,128)(2,1)}, u32[]{:S(2)}, u32[]{:S(2)}) collective-permute-start(bf16[1536,768]{1,0:T(8,128)(2,1)} %add_convert_fusion), channel_id=1, source_target_pairs={{0,1},{1,0},{2,3},{3,2},{4,5},{5,4},{6,7},{7,6},{8,9},{9,8},{10,11... | collective-permute-start | bytes 7077896 | tf_op jit(solution)/shard_map/ppermute | solution.py:157
  588.1 95.2 %all-to-all-start.7 = ((bf16[16,64,768]{2,1,0:T(8,128)(2,1)}), bf16[16,64,768]{2,1,0:T(8,128)(2,1)}, u32[]{:S(2)}, u32[]{:S(2)}) async-start(bf16[16,64,768]{2,1,0:T(8,128)(2,1)} %bitcast.240), calls=%async_computation.7 | async-start | bytes 3145728 | tf_op jit(solution)/shard_map/all_to_all | solution.py:161
  597.4 328.7 %all-reduce.4.cloned.1.call-start = ((), (), s32[]{:S(2)}) async-start(), calls=%async_computation.8 | async-start | bytes 9437184 | tf_op jit(solution)/shard_map/psum | solution.py:315
  597.7 79.2 %slice-start.6 = ((s8[4718592]{0:T(1024)(128)(4,1)}), s8[4194304]{0:T(1024)(128)(4,1)S(1)}, s32[]{:S(2)}) async-start(s8[4718592]{0:T(1024)(128)(4,1)} %bitcast.264), calls=%async_computation.15 | async-start | bytes 8388608
  600.6 76.3 %slice-start.7 = ((s8[4718592]{0:T(1024)(128)(4,1)}), s8[524288]{0:T(1024)(128)(4,1)S(1)}, s32[]{:S(2)}) async-start(s8[4718592]{0:T(1024)(128)(4,1)} %bitcast.264), calls=%async_computation.16 | async-start | bytes 1048576
  600.6 76.3 %copy-start.93 = (bf16[1024,1536]{1,0:T(8,128)(2,1)S(1)}, bf16[1024,1536]{1,0:T(8,128)(2,1)}, u32[]{:S(2)}) copy-start(bf16[1024,1536]{1,0:T(8,128)(2,1)} %copy-done.92) | copy-start | bytes 9437188
  704.3 44.7 %copy-start.34 = (bf16[768,768]{1,0:T(8,128)(2,1)S(1)}, bf16[768,768]{1,0:T(8,128)(2,1)}, u32[]{:S(2)}) copy-start(bf16[768,768]{1,0:T(8,128)(2,1)} %param.21) | copy-start | bytes 3538948
  (98 other events, 662.3 us)
Sparse Core Ops, SparseCore 0:
  776.6 149.4 all-reduce.3
